TPU v7x, 256 devices: a whole 4x4x8 slice. The times are simulated.
256 devices in a mesh: layer: 4 (over y_hi, core), latent: 64 (over x, z, y_lo).
Axes of the slice: x: 4, y: 4 (y_hi: 2, y_lo: 2; y = y_hi * 2 + y_lo), z: 8, core: 2. Of those that a mesh axis runs over, the one named last changes fastest.
Arguments:
- inputs: bfloat16 [4, 128, 4096], P('layer', 'latent'), may hold values from -6 to 6
- targets: bfloat16 [4, 128, 4096], P('layer', 'latent'), may hold values from -6 to 6
- w_enc: bfloat16 [4, 4096, 8192], P('layer', None, 'latent'), may hold values from -0.09375 to 0.09375
- b_enc: float32 [4, 8192], P('layer', 'latent'), may hold values from -3 to 3
- w_dec: bfloat16 [4, 4, 8192, 4096], P('layer', None, 'latent'), may hold values from -0.03125 to 0.03125
- b_dec: float32 [4, 4096], P('layer'), may hold values from -3 to 3
Outputs:
- grad_enc: bfloat16 [4, 4096, 8192], P('layer', None, 'latent')
- grad_benc: float32 [4, 8192], P('layer', 'latent')
- grad_dec: bfloat16 [4, 4, 8192, 4096], P('layer', None, 'latent')
- grad_bdec: float32 [4, 4096], P('layer')
All inputs are finite; a program needn't handle non-finite values.
Results may differ from a plain program's by a relative error of at most 0.0057.
Values may be sent and summed in bfloat16 or wider, within the bound.
No kernel may reach another device: no remote copies, remote signals or barrier semaphores. Data moves between devices by JAX's collectives and lax.ppermute only.
A program may use at most 64 MiB of HBM per device.

v0:
```python
import jax
import jax.numpy as jnp
from jax import lax
from jax.sharding import PartitionSpec as P

penalty = 0.5
eps = 1e-06


def sent_to_all(x, axis):
    copies = jnp.broadcast_to(x, (lax.axis_size(axis), *x.shape))
    return lax.all_to_all(copies, axis, split_axis=0, concat_axis=0, tiled=True)


def in_order(pieces, dim):
    pieces = jnp.moveaxis(pieces, 0, dim)
    lengths = pieces.shape
    return pieces.reshape(*lengths[:dim], lengths[dim] * lengths[dim + 1], *lengths[dim + 2 :])


def gather_directly(x, axis, dim):
    pieces = sent_to_all(x, axis)
    return in_order(pieces, dim)


def cut_along(x, dim, length):
    lengths = x.shape
    pieces = x.reshape(*lengths[:dim], length, lengths[dim] // length, *lengths[dim + 1 :])
    return jnp.moveaxis(pieces, dim, 0)


def summed_on_arrival(x, axis, dim):
    length = lax.axis_size(axis)
    pieces = lax.all_to_all(cut_along(x, dim, length), axis, 0, 0, tiled=True)
    return jnp.sum(pieces, axis=0)


def taken_together(x, axis):
    return sent_to_all(x, axis).sum(axis=0)


def local(inputs, targets, w_enc, b_enc, w_dec, b_dec):
    source = lax.axis_index("layer")
    depth = w_dec.shape[1]
    whole = gather_directly(inputs[0], "latent", 0)
    pre = jnp.dot(whole, w_enc[0], preferred_element_type=jnp.float32) + b_enc[0]
    positive = jnp.maximum(pre, 0.0)
    act = (positive * positive).astype(jnp.bfloat16)
    valid = (jnp.arange(depth, dtype=jnp.int32) >= source).astype(jnp.float32)
    partial_value = (
        jnp.einsum("nk,tkd->tnd", act, w_dec[0], preferred_element_type=jnp.float32)
        * valid[:, None, None]
    )
    spread = lax.psum_scatter(partial_value, "layer", scatter_dimension=0, tiled=True)
    recon = summed_on_arrival(spread, "latent", 1)
    error = recon[0] + b_dec[0] - targets[0].astype(jnp.float32)
    grad_bdec = taken_together(jnp.sum(error, axis=0), "latent")[None, :]
    err_low = error.astype(jnp.bfloat16)[None]
    stacked = gather_directly(err_low, "latent", 1)
    errors = lax.all_gather(stacked, "layer", axis=0, tiled=True)
    errors = jnp.where(valid[:, None, None] > 0.0, errors, jnp.zeros_like(errors))
    decoders = w_dec[0]
    squares = jnp.sum(jnp.square(decoders.astype(jnp.float32)), axis=2)
    norms = jnp.sqrt(jnp.sum(squares * valid[:, None], axis=0) + eps)
    back = jnp.einsum("tnd,tkd->nk", errors, decoders, preferred_element_type=jnp.float32)
    d_act = back + penalty * norms[None, :]
    d_pre = d_act * 2.0 * positive
    grad_benc = jnp.sum(d_pre, axis=0)[None, :]
    d_low = d_pre.astype(jnp.bfloat16)
    grad_enc = lax.dot_general(
        whole, d_low, (((0,), (0,)), ((), ())), preferred_element_type=jnp.float32
    ).astype(jnp.bfloat16)[None]
    act_total = jnp.sum(act.astype(jnp.float32), axis=0)
    scale = penalty * act_total / norms
    grad_mse = jnp.einsum("nk,tnd->tkd", act, errors, preferred_element_type=jnp.float32)
    shrink = valid[:, None, None] * scale[None, :, None] * decoders.astype(jnp.float32)
    grad_dec = (grad_mse + shrink).astype(jnp.bfloat16)[None]
    return (grad_enc, grad_benc, grad_dec, grad_bdec)


def solution(mesh):
    placed = (
        P("layer", "latent", None),
        P("layer", "latent", None),
        P("layer", None, "latent"),
        P("layer", "latent"),
        P("layer", None, "latent", None),
        P("layer", None),
    )
    return jax.shard_map(
        local,
        mesh=mesh,
        in_specs=placed,
        out_specs=(
            P("layer", None, "latent"),
            P("layer", "latent"),
            P("layer", None, "latent", None),
            P("layer", None),
        ),
        check_vma=False,
    )
```

profile of v0, /device:TPU:1, one launch (start us, length us, event | category | flops | bytes accessed | tf_op | source)
XLA Modules:
  0.0 318.3 jit_solution(515087838931278608)
XLA Ops:
  7.2 2.8 broadcast_in_dim.40
  10.0 13.5 %all-to-all-start = ((bf16[64,2,4096]{2,1,0:T(2,128)(2,1)}), bf16[64,2,4096]{2,1,0:T(2,128)(2,1)S(1)}, u32[]{:S(2)}, u32[]{:S(2)}) async-start(bf16[64,2,4096]{2,1,0:T(2,128)(2,1)} %broadcast_in_dim.40), calls=%async_computation | async-start | bytes 2097152 | tf_op jit(solution)/shard_map/all_to_all | solution.py:12
  23.5 0.0 reduce-scatter.2.cloned.1.call-start
  23.5 27.1 %all-to-all-done = bf16[64,2,4096]{2,1,0:T(2,128)(2,1)S(1)} async-done(((bf16[64,2,4096]{2,1,0:T(2,128)(2,1)}), bf16[64,2,4096]{2,1,0:T(2,128)(2,1)S(1)}, u32[]{:S(2)}, u32[]{:S(2)}) %all-to-all-start) | async-done | bytes 1048608 | tf_op jit(solution)/shard_map/all_to_all | solution.py:12
  50.6 0.4 reshape.76
  51.1 0.4 convert_reduce_fusion
  51.5 6.7 %multiply_bitcast_fusion = f32[4,128,4096]{2,1,0:T(8,128)} fusion(bf16[1,4,128,4096]{3,2,1,0:T(8,128)(2,1)} %param.10, f32[4]{0:T(128)S(1)} %compare_convert_fusion, f32[128,128]{1,0:T(8,128)S(1)} %get-tuple-element.29), kind=kOutput, calls=%fused_computation.5 | convolution fusion | flops 539000832 | bytes 12648464 | tf_op jit(solution)/shard_map/nk,tkd->tnd/dot_general | solution.py:51
  58.2 0.0 reduce-scatter.2.cloned.1.call-update
  58.2 0.0 all-gather.2.cloned.1.call-start
  58.3 81.5 %reduce-scatter.2.cloned.1.call-done = f32[1,128,4096]{2,1,0:T(8,128)} async-done(((f32[4,128,4096]{2,1,0:T(8,128)}), f32[1,128,4096]{2,1,0:T(8,128)}) %reduce-scatter.2.cloned.1.call-update) | async-done | bytes 2097168 | tf_op jit(solution)/shard_map/reduce_scatter | solution.py:54
  139.8 3.4 %transpose_reshape.3 = f32[64,1,2,4096]{3,2,0,1:T(2,128)} reshape(f32[1,128,4096]{2,1,0:T(8,128)} %reduce-scatter.2.cloned.1.call-done) | data formatting | bytes 4194304 | tf_op jit(solution)/shard_map/transpose;reshape | solution.py:29
  143.2 59.8 %all_to_all.21 = f32[64,1,2,4096]{3,2,1,0:T(2,128)} all-to-all(f32[64,1,2,4096]{3,2,1,0:T(2,128)} %bitcast.65), channel_id=1, replica_groups=mesh['layer'=4,'latent'=64] {'latent'}, dimensions={0} | all-to-all | bytes 4194304 | tf_op jit(solution)/shard_map/all_to_all | solution.py:34
  203.0 2.2 reduce_sum.63
  205.3 0.1 fusion.25
  205.4 1.0 broadcast_in_dim.41
  206.4 33.9 %all_to_all.22 = bf16[64,1,2,4096]{3,2,1,0:T(2,128)(2,1)S(1)} all-to-all(bf16[64,1,2,4096]{3,2,1,0:T(2,128)(2,1)S(1)} %broadcast_in_dim.41), channel_id=1, replica_groups=mesh['layer'=4,'latent'=64] {'latent'}, dimensions={0} | all-to-all | bytes 2097152 | tf_op jit(solution)/shard_map/all_to_all | solution.py:12
  240.3 1.2 reshape_transpose.3
  241.5 0.0 all-gather.2.cloned.1.call-update
  241.5 2.0 broadcast_in_dim.46
  243.5 7.5 %all-to-all-start.3 = ((f32[64,1,4096]{2,1,0:T(1,128)}), f32[64,1,4096]{2,1,0:T(1,128)S(1)}, u32[]{:S(2)}, u32[]{:S(2)}) async-start(f32[64,1,4096]{2,1,0:T(1,128)} %broadcast_in_dim.46), calls=%async_computation.4 | async-start | bytes 2097152 | tf_op jit(solution)/shard_map/all_to_all | solution.py:12
  251.0 6.5 %copy.37 = bf16[1,4,128,4096]{2,3,1,0:T(8,128)(2,1)} copy(bf16[1,4,128,4096]{3,2,1,0:T(8,128)(2,1)} %param.10) | data formatting | bytes 8388608 | tf_op args[4]
  257.5 3.0 fusion
  260.5 0.1 multiply_reduce_fusion
  260.6 0.1 broadcast_multiply_fusion
  260.7 17.0 %all-to-all-done.3 = f32[64,1,4096]{2,1,0:T(1,128)S(1)} async-done(((f32[64,1,4096]{2,1,0:T(1,128)}), f32[64,1,4096]{2,1,0:T(1,128)S(1)}, u32[]{:S(2)}, u32[]{:S(2)}) %all-to-all-start.3) | async-done | bytes 1048608 | tf_op jit(solution)/shard_map/all_to_all | solution.py:12
  277.7 1.6 reduce_sum.69
  279.2 11.7 %all-gather.2.cloned.1.call-done = bf16[4,128,4096]{2,1,0:T(8,128)(2,1)} async-done(((bf16[1,128,4096]{2,1,0:T(8,128)(2,1)}), bf16[4,128,4096]{2,1,0:T(8,128)(2,1)}) %all-gather.2.cloned.1.call-update) | async-done | bytes 4194320 | tf_op jit(solution)/shard_map/all_gather | solution.py:60
  291.0 5.3 %fusion.29 = (f32[128]{0:T(128)}, bf16[128,128]{1,0:T(8,128)(2,1)S(1)}) fusion(f32[128,128]{1,0:T(8,128)S(1)} %get-tuple-element.29, f32[128]{0:T(128)S(1)} %get-tuple-element.27, bf16[1,4,128,4096]{3,2,1,0:T(8,128)(2,1)} %param.10, bf16[4,128,4096]{2,1,0:T(8,128)(2,1)} %all-gather.2.cloned.1.call-done, pred[4]{0:T(512)(128)(4,1)S(1)} %broadcast_compare_fusion), kind=kOutput, calls=%fused_computation.36 | convolution fusion | flops 539049856 | bytes 8487940 | tf_op jit(solution)/shard_map/tnd,tkd->nk/dot_general | solution.py:65
  296.3 0.5 fusion.4
  296.7 1.3 copy.43
  298.1 7.1 %fusion.3 = bf16[1,4,128,4096]{2,3,1,0:T(8,128)(2,1)} fusion(bf16[1,4,128,4096]{2,3,1,0:T(8,128)(2,1)} %copy.37, f32[4,128]{1,0:T(4,128)S(1)} %broadcast_multiply_fusion, bf16[4,128,4096]{2,1,0:T(8,128)(2,1)} %all-gather.2.cloned.1.call-done, pred[4]{0:T(512)(128)(4,1)S(1)} %broadcast_compare_fusion, f32[128,128]{1,0:T(8,128)S(1)} %get-tuple-element.29), kind=kOutput, calls=%fused_computation.6 | convolution fusion | flops 547389440 | bytes 12650500 | tf_op jit(solution)/shard_map/nk,tnd->tkd/dot_general | solution.py:75
  305.2 6.3 %copy.44 = bf16[1,4,128,4096]{3,2,1,0:T(8,128)(2,1)} copy(bf16[1,4,128,4096]{2,3,1,0:T(8,128)(2,1)} %fusion.3) | data formatting | bytes 8388608
  (11 shorter events, 0.0 us)
Async XLA Ops:
  7.2 43.9 %copy-start = (bf16[1,4096,128]{2,1,0:T(8,128)(2,1)S(1)}, bf16[1,4096,128]{2,1,0:T(8,128)(2,1)}, u32[]{:S(2)}) copy-start(bf16[1,4096,128]{2,1,0:T(8,128)(2,1)} %param.8) | copy-start | bytes 3145732
  7.2 43.9 %copy-start.3 = (f32[1,128]{1,0:T(1,128)S(1)}, f32[1,128]{1,0:T(1,128)}, u32[]{:S(2)}) copy-start(f32[1,128]{1,0:T(1,128)} %param.9) | copy-start | bytes 1540
  10.0 40.7 %all-to-all-start = ((bf16[64,2,4096]{2,1,0:T(2,128)(2,1)}), bf16[64,2,4096]{2,1,0:T(2,128)(2,1)S(1)}, u32[]{:S(2)}, u32[]{:S(2)}) async-start(bf16[64,2,4096]{2,1,0:T(2,128)(2,1)} %broadcast_in_dim.40), calls=%async_computation | async-start | bytes 2097152 | tf_op jit(solution)/shard_map/all_to_all | solution.py:12
  23.5 116.3 %reduce-scatter.2.cloned.1.call-start = ((), (), s32[]{:S(2)}) async-start(), calls=%async_computation.5 | async-start | bytes 10485760 | tf_op jit(solution)/shard_map/reduce_scatter | solution.py:54
  58.2 232.8 %all-gather.2.cloned.1.call-start = ((), (), s32[]{:S(2)}) async-start(), calls=%async_computation.6 | async-start | bytes 5242880 | tf_op jit(solution)/shard_map/all_gather | solution.py:60
  143.2 62.1 %copy-start.1 = (bf16[1,2,4096]{2,1,0:T(2,128)(2,1)S(1)}, bf16[1,2,4096]{2,1,0:T(2,128)(2,1)}, u32[]{:S(2)}) copy-start(bf16[1,2,4096]{2,1,0:T(2,128)(2,1)} %param.7) | copy-start | bytes 49156
  143.2 62.1 %copy-start.2 = (f32[1,4096]{1,0:T(1,128)S(1)}, f32[1,4096]{1,0:T(1,128)}, u32[]{:S(2)}) copy-start(f32[1,4096]{1,0:T(1,128)} %param.11) | copy-start | bytes 49156
  243.5 34.2 %all-to-all-start.3 = ((f32[64,1,4096]{2,1,0:T(1,128)}), f32[64,1,4096]{2,1,0:T(1,128)S(1)}, u32[]{:S(2)}, u32[]{:S(2)}) async-start(f32[64,1,4096]{2,1,0:T(1,128)} %broadcast_in_dim.46), calls=%async_computation.4 | async-start | bytes 2097152 | tf_op jit(solution)/shard_map/all_to_all | solution.py:12
Sparse Core Ops, SparseCore 0:
  58.3 81.3 reduce-scatter.1
  241.6 49.3 all-gather.1
where the time goes:
time: 319 us; the launch traced here: 318 us
  waiting for transfers between devices  137 us (43%)
  blocking collectives  93.7 us (29%)
  local copies, waits for them, and re-layouts  25 us (8%)
  starting transfers between devices  21.1 us (7%)
  matrix products  20 us (6%)
  between operations  14.2 us (4%)
  other arithmetic  7.06 us (2%)
    reduce_scatter x1, waiting for transfers between devices, local(): lax.psum_scatter(partial_value, 'layer', scatter_dimension=0, tiled=True)  81.5 us
    all_to_all x1, blocking collectives, summed_on_arrival(): pieces = lax.all_to_all(cut_along(x, dim, length), axis, 0, 0, tiled=True)  59.8 us
    all_to_all x2, waiting for transfers between devices, sent_to_all(): return lax.all_to_all(copies, axis, split_axis=0, concat_axis=0, tiled=True)  44.1 us
    all_to_all x1, blocking collectives, sent_to_all(): return lax.all_to_all(copies, axis, split_axis=0, concat_axis=0, tiled=True)  33.9 us
    all_to_all x2, starting transfers between devices, sent_to_all(): return lax.all_to_all(copies, axis, split_axis=0, concat_axis=0, tiled=True)  21 us
    unnamed x11, local copies, waits for them, and re-layouts  14.2 us
    all_gather x1, waiting for transfers between devices, local(): errors = lax.all_gather(stacked, 'layer', axis=0, tiled=True)  11.7 us
    dot_general x1, matrix products, local(): jnp.einsum('nk,tnd->tkd', act, errors, preferred_element_type=jnp.float32)  7.11 us
  transfers between devices with their start and end apart: 4, of which 4 were waited for; matrix products, arithmetic and copies ran while one was open for 4% of the time, Pallas kernels for 0%

commit v1 on v0

--- a/solution.py
+++ b/solution.py
@@ -57,7 +57,9 @@
     grad_bdec = taken_together(jnp.sum(error, axis=0), "latent")[None, :]
     err_low = error.astype(jnp.bfloat16)[None]
     stacked = gather_directly(err_low, "latent", 1)
-    errors = lax.all_gather(stacked, "layer", axis=0, tiled=True)
+    errors = jnp.concatenate(
+        lax.all_to_all(jnp.stack([stacked] * lax.axis_size("layer")), "layer", 0, 0), axis=0
+    )
     errors = jnp.where(valid[:, None, None] > 0.0, errors, jnp.zeros_like(errors))
     decoders = w_dec[0]
     squares = jnp.sum(jnp.square(decoders.astype(jnp.float32)), axis=2)

time: 319 us -> 364 us (1.14)
  waiting for transfers between devices: 137 us -> 169 us
  starting transfers between devices: 21.1 us -> 28.8 us
  local copies, waits for them, and re-layouts: 25 us -> 29 us
    all_to_all x0 -> x1, waiting for transfers between devices: none -> 36.6 us  [local(): lax.all_to_all(jnp.stack([stacked] * lax.axis_size('layer')), 'layer', 0, 0)]
    all_gather x1 -> x0, waiting for transfers between devices: 11.7 us -> none  [local(): errors = lax.all_gather(stacked, 'layer', axis=0, tiled=True)]
    all_to_all x0 -> x1, starting transfers between devices: none -> 7.75 us  [local(): lax.all_to_all(jnp.stack([stacked] * lax.axis_size('layer')), 'layer', 0, 0)]
    all_to_all x2, waiting for transfers between devices: 44.1 us -> 51 us  [sent_to_all(): return lax.all_to_all(copies, axis, split_axis=0, concat_axis=0, tiled=True)]
    another operation x1 -> x3, local copies, waits for them, and re-layouts: 1.2 us -> 5.34 us  [local(): jnp.stack([stacked] * lax.axis_size('layer'))]
where the time goes in v1:
time: 364 us; the launch traced here: 363 us
  waiting for transfers between devices  169 us (46%)
  blocking collectives  93.7 us (26%)
  local copies, waits for them, and re-layouts  29 us (8%)
  starting transfers between devices  28.8 us (8%)
  matrix products  19.9 us (5%)
  between operations  14.2 us (4%)
  other arithmetic  8.17 us (2%)
    reduce_scatter x1, waiting for transfers between devices, local(): lax.psum_scatter(partial_value, 'layer', scatter_dimension=0, tiled=True)  81.5 us
    all_to_all x1, blocking collectives, summed_on_arrival(): pieces = lax.all_to_all(cut_along(x, dim, length), axis, 0, 0, tiled=True)  59.8 us
    all_to_all x2, waiting for transfers between devices, sent_to_all(): return lax.all_to_all(copies, axis, split_axis=0, concat_axis=0, tiled=True)  51 us
    all_to_all x1, waiting for transfers between devices, local(): lax.all_to_all(jnp.stack([stacked] * lax.axis_size('layer')), 'layer', 0, 0)  36.6 us
    all_to_all x1, blocking collectives, sent_to_all(): return lax.all_to_all(copies, axis, split_axis=0, concat_axis=0, tiled=True)  33.9 us
    all_to_all x2, starting transfers between devices, sent_to_all(): return lax.all_to_all(copies, axis, split_axis=0, concat_axis=0, tiled=True)  21.1 us
    unnamed x11, local copies, waits for them, and re-layouts  14 us
    all_to_all x1, starting transfers between devices, local(): lax.all_to_all(jnp.stack([stacked] * lax.axis_size('layer')), 'layer', 0, 0)  7.75 us
  transfers between devices with their start and end apart: 4, of which 4 were waited for; matrix products, arithmetic and copies ran while one was open for 4% of the time, Pallas kernels for 0%

profile of v1, /device:TPU:1, one launch (start us, length us, event | category | flops | bytes accessed | tf_op | source)
XLA Modules:
  0.0 362.9 jit_solution(492186709906087559)
XLA Ops:
  7.2 2.8 broadcast_in_dim.40
  10.0 13.5 %all-to-all-start = ((bf16[64,2,4096]{2,1,0:T(2,128)(2,1)}), bf16[64,2,4096]{2,1,0:T(2,128)(2,1)S(1)}, u32[]{:S(2)}, u32[]{:S(2)}) async-start(bf16[64,2,4096]{2,1,0:T(2,128)(2,1)} %broadcast_in_dim.40), calls=%async_computation | async-start | bytes 2097152 | tf_op jit(solution)/shard_map/all_to_all | solution.py:12
  23.5 0.0 reduce-scatter.2.cloned.1.call-start
  23.5 27.1 %all-to-all-done = bf16[64,2,4096]{2,1,0:T(2,128)(2,1)S(1)} async-done(((bf16[64,2,4096]{2,1,0:T(2,128)(2,1)}), bf16[64,2,4096]{2,1,0:T(2,128)(2,1)S(1)}, u32[]{:S(2)}, u32[]{:S(2)}) %all-to-all-start) | async-done | bytes 1048608 | tf_op jit(solution)/shard_map/all_to_all | solution.py:12
  50.6 0.4 reshape.83
  51.1 0.4 convert_reduce_fusion
  51.5 6.7 %multiply_bitcast_fusion = f32[4,128,4096]{2,1,0:T(8,128)} fusion(bf16[1,4,128,4096]{3,2,1,0:T(8,128)(2,1)} %param.10, f32[4]{0:T(128)S(1)} %compare_convert_fusion, f32[128,128]{1,0:T(8,128)S(1)} %get-tuple-element.29), kind=kOutput, calls=%fused_computation.5 | convolution fusion | flops 539000832 | bytes 12648464 | tf_op jit(solution)/shard_map/nk,tkd->tnd/dot_general | solution.py:51
  58.2 81.5 %reduce-scatter.2.cloned.1.call-done = f32[1,128,4096]{2,1,0:T(8,128)} async-done(((f32[4,128,4096]{2,1,0:T(8,128)}), f32[1,128,4096]{2,1,0:T(8,128)}) %reduce-scatter.2.cloned.1.call-update) | async-done | bytes 2097168 | tf_op jit(solution)/shard_map/reduce_scatter | solution.py:54
  139.8 3.4 transpose_reshape.3
  143.2 59.8 %all_to_all.26 = f32[64,1,2,4096]{3,2,1,0:T(2,128)} all-to-all(f32[64,1,2,4096]{3,2,1,0:T(2,128)} %bitcast.79), channel_id=1, replica_groups=mesh['layer'=4,'latent'=64] {'latent'}, dimensions={0} | all-to-all | bytes 4194304 | tf_op jit(solution)/shard_map/all_to_all | solution.py:34
  203.0 2.2 reduce_sum.63
  205.3 0.1 fusion.25
  205.4 1.0 broadcast_in_dim.41
  206.4 33.9 %all_to_all.27 = bf16[64,1,2,4096]{3,2,1,0:T(2,128)(2,1)S(1)} all-to-all(bf16[64,1,2,4096]{3,2,1,0:T(2,128)(2,1)S(1)} %broadcast_in_dim.41), channel_id=1, replica_groups=mesh['layer'=4,'latent'=64] {'latent'}, dimensions={0} | all-to-all | bytes 2097152 | tf_op jit(solution)/shard_map/all_to_all | solution.py:12
  240.3 2.0 broadcast_in_dim.46
  242.3 7.6 %all-to-all-start.4 = ((f32[64,1,4096]{2,1,0:T(1,128)}), f32[64,1,4096]{2,1,0:T(1,128)}, u32[]{:S(2)}, u32[]{:S(2)}) async-start(f32[64,1,4096]{2,1,0:T(1,128)} %broadcast_in_dim.46), calls=%async_computation.5 | async-start | bytes 2097152 | tf_op jit(solution)/shard_map/all_to_all | solution.py:12
  249.8 1.2 stack_reshape_transpose.2
  251.0 1.6 copy.43
  252.7 23.9 %all-to-all-done.4 = f32[64,1,4096]{2,1,0:T(1,128)} async-done(((f32[64,1,4096]{2,1,0:T(1,128)}), f32[64,1,4096]{2,1,0:T(1,128)}, u32[]{:S(2)}, u32[]{:S(2)}) %all-to-all-start.4) | async-done | bytes 1048608 | tf_op jit(solution)/shard_map/all_to_all | solution.py:12
  276.5 2.5 stack.3
  279.0 7.8 %all-to-all-start.3 = ((bf16[4,1,128,4096]{2,3,1,0:T(8,128)(2,1)}), bf16[4,1,128,4096]{2,3,1,0:T(8,128)(2,1)}, u32[]{:S(2)}, u32[]{:S(2)}) async-start(bf16[4,1,128,4096]{2,3,1,0:T(8,128)(2,1)} %stack.3), calls=%async_computation.4 | async-start | bytes 8388608 | tf_op jit(solution)/shard_map/all_to_all | solution.py:61
  286.8 6.3 %copy.40 = bf16[1,4,128,4096]{2,3,1,0:T(8,128)(2,1)} copy(bf16[1,4,128,4096]{3,2,1,0:T(8,128)(2,1)} %param.10) | data formatting | bytes 8388608 | tf_op args[4]
  293.1 3.0 fusion
  296.1 0.1 multiply_reduce_fusion
  296.2 0.1 broadcast_multiply_fusion
  296.3 2.7 reduce_sum.69
  299.0 36.6 %all-to-all-done.3 = bf16[4,1,128,4096]{2,3,1,0:T(8,128)(2,1)} async-done(((bf16[4,1,128,4096]{2,3,1,0:T(8,128)(2,1)}), bf16[4,1,128,4096]{2,3,1,0:T(8,128)(2,1)}, u32[]{:S(2)}, u32[]{:S(2)}) %all-to-all-start.3) | async-done | bytes 4194336 | tf_op jit(solution)/shard_map/all_to_all | solution.py:61
  335.6 5.5 %fusion.29 = (f32[128]{0:T(128)}, bf16[128,128]{1,0:T(8,128)(2,1)S(1)}) fusion(f32[128,128]{1,0:T(8,128)S(1)} %get-tuple-element.29, f32[128]{0:T(128)S(1)} %get-tuple-element.27, bf16[1,4,128,4096]{3,2,1,0:T(8,128)(2,1)} %param.10, bf16[4,1,128,4096]{2,3,1,0:T(8,128)(2,1)} %all-to-all-done.3, pred[4]{0:T(512)(128)(4,1)S(1)} %broadcast_compare_fusion), kind=kOutput, calls=%fused_computation.36 | convolution fusion | flops 539049856 | bytes 8487940 | tf_op jit(solution)/shard_map/tnd,tkd->nk/dot_general | solution.py:67
  341.1 0.5 fusion.4
  341.5 1.3 copy.47
  342.8 6.8 %fusion.3 = bf16[1,4,128,4096]{2,3,1,0:T(8,128)(2,1)} fusion(bf16[1,4,128,4096]{2,3,1,0:T(8,128)(2,1)} %copy.40, f32[4,128]{1,0:T(4,128)S(1)} %broadcast_multiply_fusion, bf16[4,1,128,4096]{2,3,1,0:T(8,128)(2,1)} %all-to-all-done.3, pred[4]{0:T(512)(128)(4,1)S(1)} %broadcast_compare_fusion, f32[128,128]{1,0:T(8,128)S(1)} %get-tuple-element.29), kind=kOutput, calls=%fused_computation.6 | convolution fusion | flops 547389440 | bytes 12650500 | tf_op jit(solution)/shard_map/nk,tnd->tkd/dot_general | solution.py:77
  349.7 6.3 %copy.48 = bf16[1,4,128,4096]{3,2,1,0:T(8,128)(2,1)} copy(bf16[1,4,128,4096]{2,3,1,0:T(8,128)(2,1)} %fusion.3) | data formatting | bytes 8388608
  (12 shorter events, 0.1 us)
Async XLA Ops:
  7.2 43.9 %copy-start = (bf16[1,4096,128]{2,1,0:T(8,128)(2,1)S(1)}, bf16[1,4096,128]{2,1,0:T(8,128)(2,1)}, u32[]{:S(2)}) copy-start(bf16[1,4096,128]{2,1,0:T(8,128)(2,1)} %param.8) | copy-start | bytes 3145732
  7.2 43.9 %copy-start.3 = (f32[1,128]{1,0:T(1,128)S(1)}, f32[1,128]{1,0:T(1,128)}, u32[]{:S(2)}) copy-start(f32[1,128]{1,0:T(1,128)} %param.9) | copy-start | bytes 1540
  10.0 40.7 %all-to-all-start = ((bf16[64,2,4096]{2,1,0:T(2,128)(2,1)}), bf16[64,2,4096]{2,1,0:T(2,128)(2,1)S(1)}, u32[]{:S(2)}, u32[]{:S(2)}) async-start(bf16[64,2,4096]{2,1,0:T(2,128)(2,1)} %broadcast_in_dim.40), calls=%async_computation | async-start | bytes 2097152 | tf_op jit(solution)/shard_map/all_to_all | solution.py:12
  23.5 116.3 %reduce-scatter.2.cloned.1.call-start = ((), (), s32[]{:S(2)}) async-start(), calls=%async_computation.6 | async-start | bytes 10485760 | tf_op jit(solution)/shard_map/reduce_scatter | solution.py:54
  143.2 62.1 %copy-start.1 = (bf16[1,2,4096]{2,1,0:T(2,128)(2,1)S(1)}, bf16[1,2,4096]{2,1,0:T(2,128)(2,1)}, u32[]{:S(2)}) copy-start(bf16[1,2,4096]{2,1,0:T(2,128)(2,1)} %param.7) | copy-start | bytes 49156
  143.2 62.1 %copy-start.2 = (f32[1,4096]{1,0:T(1,128)S(1)}, f32[1,4096]{1,0:T(1,128)}, u32[]{:S(2)}) copy-start(f32[1,4096]{1,0:T(1,128)} %param.11) | copy-start | bytes 49156
  242.3 34.3 %all-to-all-start.4 = ((f32[64,1,4096]{2,1,0:T(1,128)}), f32[64,1,4096]{2,1,0:T(1,128)}, u32[]{:S(2)}, u32[]{:S(2)}) async-start(f32[64,1,4096]{2,1,0:T(1,128)} %broadcast_in_dim.46), calls=%async_computation.5 | async-start | bytes 2097152 | tf_op jit(solution)/shard_map/all_to_all | solution.py:12
  279.0 56.5 %all-to-all-start.3 = ((bf16[4,1,128,4096]{2,3,1,0:T(8,128)(2,1)}), bf16[4,1,128,4096]{2,3,1,0:T(8,128)(2,1)}, u32[]{:S(2)}, u32[]{:S(2)}) async-start(bf16[4,1,128,4096]{2,3,1,0:T(8,128)(2,1)} %stack.3), calls=%async_computation.4 | async-start | bytes 8388608 | tf_op jit(solution)/shard_map/all_to_all | solution.py:61
Sparse Core Ops, SparseCore 0:
  58.3 81.3 reduce-scatter.1
